TPU v7x, 32 devices: a whole 2x2x4 slice. The times are simulated.
32 devices in a mesh: section: 4 (over z), gx: 2 (over x), gy: 2 (over y), gz: 2 (over core).
Axes of the slice: x: 2, y: 2, z: 4, core: 2. Of those that a mesh axis runs over, the one named last changes fastest.
Arguments:
- micro_inputs: bfloat16 [1, 256, 8192], P(None, 'gy', ('gx', 'gz')), may hold values from -40 to 40
- norm_gain: float32 [4, 8192], P('section', 'gx'), may hold values from 0.5 to 1.5
- q_weight: bfloat16 [4, 8192, 8192], P('section', ('gx', 'gy'), 'gz'), may hold values from -0.0625 to 0.0625
- kv_weight: bfloat16 [4, 2, 8192, 1024], P('section', None, ('gx', 'gy'), 'gz'), may hold values from -0.0625 to 0.0625
- q_bias: float32 [4, 8192], P('section', 'gz'), may hold values from -130 to 130
- kv_bias: float32 [4, 2, 1024], P('section', None, 'gz'), may hold values from -50 to 50
- out_weight: bfloat16 [4, 8192, 8192], P('section', 'gz', ('gx', 'gy')), may hold values from -0.0625 to 0.0625
Outputs:
- hidden_out: bfloat16 [4, 1, 256, 8192], P('section', None, 'gy', ('gx', 'gz'))
All inputs are finite; a program needn't handle non-finite values.
Results may differ from a plain program's by a relative error of at most 0.025.
Values may be sent and summed in bfloat16 or wider, within the bound.
No kernel may reach another device: no remote copies, remote signals or barrier semaphores. Data moves between devices by JAX's collectives and lax.ppermute only.
A program may use at most 128 MiB of HBM per device.

v0:
```python
import jax
import jax.numpy as jnp
from jax import lax
from jax.sharding import PartitionSpec as P

D = 8192
HD = 128
ROPE_BASE = 1000000.0
EPSILON = 1e-06
NEG_FILL = -1e30


def from_behind(value, axis, steps):
    count = lax.axis_size(axis)
    initial, last = (max(0, -steps), min(count, count - steps))
    return lax.ppermute(value, axis, [(source, source + steps) for source in range(initial, last)])


def rotary(values, positions):
    half_width = values.shape[-1] // 2
    frequency = ROPE_BASE ** (-jnp.arange(half_width, dtype=jnp.float32) * 2.0 / values.shape[-1])
    angles = positions.astype(jnp.float32)[:, None] * frequency[None, :]
    cosine = jnp.cos(angles)[:, None, :]
    sine_part = jnp.sin(angles)[:, None, :]
    lower_half = values[..., :half_width]
    upper_half = values[..., half_width:]
    return jnp.concatenate(
        [
            lower_half * cosine - upper_half * sine_part,
            upper_half * cosine + lower_half * sine_part,
        ],
        axis=-1,
    )


def body(micro_inputs, norm_gain, q_weight, kv_weight, q_bias, kv_bias, out_weight):
    section_count = lax.axis_size("section")
    size_gx = lax.axis_size("gx")
    micro_count = micro_inputs.shape[0]
    local_rows = micro_inputs.shape[1]
    index_gx = lax.axis_index("gx")
    index_gy = lax.axis_index("gy")
    index_section = lax.axis_index("section")
    query_weight = q_weight[0]
    pair_weight = jnp.concatenate([kv_weight[0, 0], kv_weight[0, 1]], axis=1)
    mixing_weight = out_weight[0]
    slab_rows = q_weight.shape[1]
    q_cols = query_weight.shape[1]
    kv_cols = pair_weight.shape[1] // 2
    gain_row = norm_gain[0]
    q_heads = q_cols // HD
    kv_heads = kv_cols // HD
    group_size = q_heads // kv_heads
    own_cols = q_cols // size_gx
    own_heads = own_cols // HD
    if own_heads > group_size:
        used_heads = own_heads // group_size
        local_group = group_size
    else:
        used_heads = 1
        local_group = own_heads
    used_start = index_gx * own_heads // group_size
    score_scale = HD ** (-0.5)
    row_pos = index_gy * local_rows + jnp.arange(local_rows)
    own_bias = lax.dynamic_slice_in_dim(q_bias[0], index_gx * own_cols, own_cols, 0)

    def mix_cols(piece):
        return jnp.dot(piece, mixing_weight, preferred_element_type=jnp.float32)

    def attention_layer(wide_block):
        widened = wide_block.astype(jnp.float32)
        squares = lax.psum(jnp.sum(widened * widened, axis=1), "gx")
        normed = (widened * lax.rsqrt(squares / D + EPSILON)[:, None] * gain_row[None, :]).astype(
            jnp.bfloat16
        )
        all_tokens = lax.all_gather(normed, "gy", axis=0, tiled=True)
        own_slab = lax.dynamic_slice_in_dim(all_tokens, index_gy * slab_rows, slab_rows, 1)
        query_part = jnp.dot(own_slab, query_weight, preferred_element_type=jnp.float32)
        pair_part = jnp.dot(own_slab, pair_weight, preferred_element_type=jnp.float32)
        query_rows, pair_local = (
            lax.psum_scatter(
                query_part.astype(jnp.bfloat16), "gy", scatter_dimension=0, tiled=True
            ).astype(jnp.float32),
            lax.psum_scatter(
                pair_part.astype(jnp.bfloat16), "gy", scatter_dimension=0, tiled=True
            ).astype(jnp.float32),
        )
        queries = (
            lax.psum_scatter(
                query_rows.astype(jnp.bfloat16), "gx", scatter_dimension=1, tiled=True
            ).astype(jnp.float32)
            + own_bias[None, :]
        )
        pair_terms = lax.psum(pair_local.astype(jnp.bfloat16), "gx").astype(jnp.float32)
        key_rows = pair_terms[:, :kv_cols] + kv_bias[0, 0][None, :]
        value_rows = (pair_terms[:, kv_cols:] + kv_bias[0, 1][None, :]).astype(jnp.bfloat16)
        queries = rotary(queries.reshape(local_rows, own_heads, HD), row_pos).astype(jnp.bfloat16)
        queries = queries.reshape(local_rows, used_heads, local_group, HD)
        key_rows = rotary(key_rows.reshape(local_rows, kv_heads, HD), row_pos).astype(jnp.bfloat16)
        key_used = lax.dynamic_slice_in_dim(key_rows, used_start, used_heads, 1).reshape(
            local_rows, used_heads * HD
        )
        value_used = lax.dynamic_slice_in_dim(
            value_rows.reshape(local_rows, kv_heads, HD), used_start, used_heads, 1
        ).reshape(local_rows, used_heads * HD)
        running_max = jnp.full((used_heads, local_group, local_rows), NEG_FILL, jnp.float32)
        key_piece = lax.all_gather(key_used, "gy", axis=0, tiled=True)
        value_piece = lax.all_gather(value_used, "gy", axis=0, tiled=True)
        key_count = key_piece.shape[0]
        key_pos = jnp.arange(key_count)
        scores = (
            jnp.einsum(
                "qhgd,khd->hgqk",
                queries,
                key_piece.reshape(key_count, used_heads, HD),
                preferred_element_type=jnp.float32,
            )
            * score_scale
        )
        allowed = key_pos[None, :] <= row_pos[:, None]
        scores = jnp.where(allowed, scores, NEG_FILL)
        new_max = jnp.maximum(running_max, jnp.max(scores, axis=-1))
        weights = jnp.where(allowed, jnp.exp(scores - new_max[..., None]), 0.0)
        running_sum = jnp.sum(weights, axis=-1)
        update = jnp.einsum(
            "hgqk,khd->qhgd",
            weights.astype(jnp.bfloat16),
            value_piece.reshape(key_count, used_heads, HD),
            preferred_element_type=jnp.float32,
        )
        weighted = update
        running_max, running_sum, weighted = (new_max, running_sum, weighted)
        attended = (
            (weighted / jnp.transpose(running_sum, (2, 0, 1))[..., None])
            .astype(jnp.bfloat16)
            .reshape(local_rows, own_cols)
        )
        every_token = lax.all_gather(attended, "gy", axis=0, tiled=True)
        column_sums = mix_cols(lax.all_gather(every_token, "gx", axis=1, tiled=True))
        return lax.all_to_all(
            column_sums.astype(jnp.bfloat16), "gy", split_axis=0, concat_axis=1, tiled=True
        ).astype(column_sums.dtype)

    def record(stored, tick_index, result):
        micro_index = tick_index - index_section
        is_valid = (micro_index >= 0) & (micro_index < micro_count)
        clipped = jnp.clip(micro_index, 0, micro_count - 1)
        previous = lax.dynamic_index_in_dim(stored, clipped, 0, keepdims=False)
        return lax.dynamic_update_index_in_dim(
            stored, jnp.where(is_valid, result, previous), clipped, 0
        )

    tick_count = micro_count + section_count - 1
    stored_start = jnp.zeros(micro_inputs.shape, jnp.bfloat16)

    def advance(tick_index, state):
        carried, stored = state
        fresh = lax.dynamic_index_in_dim(
            micro_inputs, jnp.clip(tick_index, 0, micro_count - 1), 0, keepdims=False
        )
        current = jnp.where(index_section == 0, fresh, carried)
        wide_block = lax.all_gather(current, "gz", axis=1, tiled=True)
        summed = lax.psum_scatter(
            attention_layer(wide_block).astype(jnp.bfloat16), "gz", scatter_dimension=1, tiled=True
        ).astype(jnp.float32)
        result = (current.astype(jnp.float32) + summed).astype(jnp.bfloat16)
        stored = record(stored, tick_index, result)
        return (from_behind(result, "section", 1), stored)

    carry_start = jnp.zeros(micro_inputs.shape[1:], jnp.bfloat16)
    final_state = lax.fori_loop(0, tick_count, advance, (carry_start, stored_start))
    return final_state[1][None]


def solution(mesh):
    return jax.shard_map(
        body,
        mesh=mesh,
        in_specs=(
            P(None, "gy", ("gx", "gz")),
            P("section", "gx"),
            P("section", ("gx", "gy"), "gz"),
            P("section", None, ("gx", "gy"), "gz"),
            P("section", "gz"),
            P("section", None, "gz"),
            P("section", "gz", ("gx", "gy")),
        ),
        out_specs=P("section", None, "gy", ("gx", "gz")),
        check_vma=False,
    )
```

profile of v0, /device:TPU:0, one launch (start us, length us, event | category | flops | bytes accessed | tf_op | source)
XLA Modules:
  0.0 1107.2 jit_solution(5537659410085549743)
XLA Ops:
  12.5 1087.3 %while.19 = (s32[]{:T(128)}, bf16[128,2048]{1,0:T(8,128)(2,1)S(1)}, bf16[1,128,2048]{2,1,0:T(8,128)(2,1)S(1)}, pred[]{:T(512)}, bf16[1,128,2048]{2,1,0:T(8,128)(...) while((s32[]{:T(128)}, bf16[128,2048]{1,0:T(8,128)(2,1)S(1)}, ...), condition=%wide.region_10.11_spmd.clone.clone, body=%wide.region_0.10_spmd.clone.clone.sunk | while | flops 9950043136 | bytes 130518144 | solution.py:171
  13.5 13.2 %all-gather.5.cloned.1.call-done = bf16[128,4096]{1,0:T(8,128)(2,1)} async-done(((bf16[128,2048]{1,0:T(8,128)(2,1)}), bf16[128,4096]{1,0:T(8,128)(2,1)}) %all-gather.5.cloned.1.call-update) | async-done | bytes 1048592 | tf_op jit(solution)/shard_map/while/body/eval_jaxpr/all_gather | solution.py:162
  28.2 4.9 psum.34
  35.8 34.4 %all-gather.7.cloned.1.call-done = bf16[256,4096]{1,0:T(8,128)(2,1)} async-done(((bf16[128,4096]{1,0:T(8,128)(2,1)}), bf16[256,4096]{1,0:T(8,128)(2,1)}) %all-gather.7.cloned.1.call-update) | async-done | bytes 2097168 | tf_op jit(solution)/shard_map/while/body/eval_jaxpr/all_gather | solution.py:76
  70.2 4.6 convolution_convert_fusion.6
  74.8 12.0 %convolution_convert_fusion.7 = bf16[256,4096]{1,0:T(8,128)(2,1)} fusion(bf16[2048,4096]{1,0:T(8,128)(2,1)} %get-tuple-element.638, bf16[256,4096]{1,0:T(8,128)(2,1)} %all-gather.7.cloned.1.call-done, s32[]{:T(128)} %get-tuple-element.634), kind=kOutput, calls=%fused_computation.2.clone.1 | convolution fusion | flops 4296015872 | bytes 19923456 | tf_op jit(solution)/shard_map/while/body/eval_jaxpr/dot_general | solution.py:78
  89.7 34.0 %reduce-scatter.7.cloned.1.call-done = bf16[128,4096]{1,0:T(8,128)(2,1)} async-done(((bf16[256,4096]{1,0:T(8,128)(2,1)}), bf16[128,4096]{1,0:T(8,128)(2,1)}) %reduce-scatter.7.cloned.1.call-update) | async-done | bytes 1048592 | tf_op jit(solution)/shard_map/while/body/eval_jaxpr/reduce_scatter | solution.py:81
  124.1 25.0 %all-reduce.2.cloned.1.call-done = bf16[128,1024]{1,0:T(8,128)(2,1)} async-done(((bf16[128,1024]{1,0:T(8,128)(2,1)}), bf16[128,1024]{1,0:T(8,128)(2,1)}) %all-reduce.2.cloned.1.call-update) | async-done | bytes 262160 | tf_op jit(solution)/shard_map/while/body/eval_jaxpr/psum | solution.py:94
  151.0 5.0 all_gather.81
  156.0 5.0 all_gather.80
  161.0 10.6 reduce-scatter.9.cloned.1.call-done
  176.5 21.4 %all-gather.9.cloned.1.call-done = bf16[256,2048]{0,1:T(8,128)(2,1)} async-done(((bf16[128,2048]{0,1:T(8,128)(2,1)}), bf16[256,2048]{0,1:T(8,128)(2,1)}) %all-gather.9.cloned.1.call-update) | async-done | bytes 1048592 | tf_op jit(solution)/shard_map/while/body/eval_jaxpr/all_gather | solution.py:138
  197.9 34.6 %all-gather.11.cloned.1.call-done = bf16[256,4096]{0,1:T(8,128)(2,1)} async-done(((bf16[256,2048]{0,1:T(8,128)(2,1)}), bf16[256,4096]{0,1:T(8,128)(2,1)}) %all-gather.11.cloned.1.call-update) | async-done | bytes 2097168 | tf_op jit(solution)/shard_map/while/body/eval_jaxpr/all_gather | solution.py:139
  232.5 10.9 convolution_convert_fusion.8
  243.5 16.2 %all_to_all.48 = bf16[2,128,2048]{2,1,0:T(8,128)(2,1)S(1)} all-to-all(bf16[2,128,2048]{2,1,0:T(8,128)(2,1)S(1)} %bitcast.132), channel_id=1, replica_groups=mesh['section'=4,'gx'=2,'gy'=2,'gz'=2] {'gy'}, dimensions={0} | all-to-all | bytes 2097152 | tf_op jit(solution)/shard_map/while/body/eval_jaxpr/all_to_all | solution.py:140
  260.7 7.6 reduce-scatter.11.cloned.1.call-done
  273.4 11.6 %collective-permute-done = bf16[128,2048]{1,0:T(8,128)(2,1)S(1)} collective-permute-done((bf16[128,2048]{1,0:T(8,128)(2,1)S(1)}, bf16[128,2048]{1,0:T(8,128)(2,1)S(1)}, u32[]{:S(2)}, u32[]{:S(2)}) %collective-permute-start) | collective-permute-done | bytes 524320 | tf_op jit(solution)/shard_map/while/body/eval_jaxpr/ppermute | solution.py:16
  285.9 12.1 %all-gather.5.cloned.1.call-done = bf16[128,4096]{1,0:T(8,128)(2,1)} async-done(((bf16[128,2048]{1,0:T(8,128)(2,1)}), bf16[128,4096]{1,0:T(8,128)(2,1)}) %all-gather.5.cloned.1.call-update) | async-done | bytes 1048592 | tf_op jit(solution)/shard_map/while/body/eval_jaxpr/all_gather | solution.py:162
  299.5 4.9 psum.34
  307.0 34.4 %all-gather.7.cloned.1.call-done = bf16[256,4096]{1,0:T(8,128)(2,1)} async-done(((bf16[128,4096]{1,0:T(8,128)(2,1)}), bf16[256,4096]{1,0:T(8,128)(2,1)}) %all-gather.7.cloned.1.call-update) | async-done | bytes 2097168 | tf_op jit(solution)/shard_map/while/body/eval_jaxpr/all_gather | solution.py:76
  346.1 12.0 %convolution_convert_fusion.7 = bf16[256,4096]{1,0:T(8,128)(2,1)} fusion(bf16[2048,4096]{1,0:T(8,128)(2,1)} %get-tuple-element.638, bf16[256,4096]{1,0:T(8,128)(2,1)} %all-gather.7.cloned.1.call-done, s32[]{:T(128)} %get-tuple-element.634), kind=kOutput, calls=%fused_computation.2.clone.1 | convolution fusion | flops 4296015872 | bytes 19923456 | tf_op jit(solution)/shard_map/while/body/eval_jaxpr/dot_general | solution.py:78
  360.9 34.1 %reduce-scatter.7.cloned.1.call-done = bf16[128,4096]{1,0:T(8,128)(2,1)} async-done(((bf16[256,4096]{1,0:T(8,128)(2,1)}), bf16[128,4096]{1,0:T(8,128)(2,1)}) %reduce-scatter.7.cloned.1.call-update) | async-done | bytes 1048592 | tf_op jit(solution)/shard_map/while/body/eval_jaxpr/reduce_scatter | solution.py:81
  395.5 25.0 %all-reduce.2.cloned.1.call-done = bf16[128,1024]{1,0:T(8,128)(2,1)} async-done(((bf16[128,1024]{1,0:T(8,128)(2,1)}), bf16[128,1024]{1,0:T(8,128)(2,1)}) %all-reduce.2.cloned.1.call-update) | async-done | bytes 262160 | tf_op jit(solution)/shard_map/while/body/eval_jaxpr/psum | solution.py:94
  422.5 5.0 all_gather.81
  427.4 5.0 all_gather.80
  432.4 10.6 reduce-scatter.9.cloned.1.call-done
  447.9 21.4 %all-gather.9.cloned.1.call-done = bf16[256,2048]{0,1:T(8,128)(2,1)} async-done(((bf16[128,2048]{0,1:T(8,128)(2,1)}), bf16[256,2048]{0,1:T(8,128)(2,1)}) %all-gather.9.cloned.1.call-update) | async-done | bytes 1048592 | tf_op jit(solution)/shard_map/while/body/eval_jaxpr/all_gather | solution.py:138
  469.4 34.4 %all-gather.11.cloned.1.call-done = bf16[256,4096]{0,1:T(8,128)(2,1)} async-done(((bf16[256,2048]{0,1:T(8,128)(2,1)}), bf16[256,4096]{0,1:T(8,128)(2,1)}) %all-gather.11.cloned.1.call-update) | async-done | bytes 2097168 | tf_op jit(solution)/shard_map/while/body/eval_jaxpr/all_gather | solution.py:139
  503.8 10.9 convolution_convert_fusion.8
  514.7 16.2 %all_to_all.48 = bf16[2,128,2048]{2,1,0:T(8,128)(2,1)S(1)} all-to-all(bf16[2,128,2048]{2,1,0:T(8,128)(2,1)S(1)} %bitcast.132), channel_id=1, replica_groups=mesh['section'=4,'gx'=2,'gy'=2,'gz'=2] {'gy'}, dimensions={0} | all-to-all | bytes 2097152 | tf_op jit(solution)/shard_map/while/body/eval_jaxpr/all_to_all | solution.py:140
  532.0 7.6 reduce-scatter.11.cloned.1.call-done
  544.6 11.6 %collective-permute-done = bf16[128,2048]{1,0:T(8,128)(2,1)S(1)} collective-permute-done((bf16[128,2048]{1,0:T(8,128)(2,1)S(1)}, bf16[128,2048]{1,0:T(8,128)(2,1)S(1)}, u32[]{:S(2)}, u32[]{:S(2)}) %collective-permute-start) | collective-permute-done | bytes 524320 | tf_op jit(solution)/shard_map/while/body/eval_jaxpr/ppermute | solution.py:16
  557.1 12.4 %all-gather.5.cloned.1.call-done = bf16[128,4096]{1,0:T(8,128)(2,1)} async-done(((bf16[128,2048]{1,0:T(8,128)(2,1)}), bf16[128,4096]{1,0:T(8,128)(2,1)}) %all-gather.5.cloned.1.call-update) | async-done | bytes 1048592 | tf_op jit(solution)/shard_map/while/body/eval_jaxpr/all_gather | solution.py:162
  571.1 4.9 psum.34
  578.6 34.4 %all-gather.7.cloned.1.call-done = bf16[256,4096]{1,0:T(8,128)(2,1)} async-done(((bf16[128,4096]{1,0:T(8,128)(2,1)}), bf16[256,4096]{1,0:T(8,128)(2,1)}) %all-gather.7.cloned.1.call-update) | async-done | bytes 2097168 | tf_op jit(solution)/shard_map/while/body/eval_jaxpr/all_gather | solution.py:76
  613.0 4.6 convolution_convert_fusion.6
  617.7 12.0 %convolution_convert_fusion.7 = bf16[256,4096]{1,0:T(8,128)(2,1)} fusion(bf16[2048,4096]{1,0:T(8,128)(2,1)} %get-tuple-element.638, bf16[256,4096]{1,0:T(8,128)(2,1)} %all-gather.7.cloned.1.call-done, s32[]{:T(128)} %get-tuple-element.634), kind=kOutput, calls=%fused_computation.2.clone.1 | convolution fusion | flops 4296015872 | bytes 19923456 | tf_op jit(solution)/shard_map/while/body/eval_jaxpr/dot_general | solution.py:78
  632.5 34.1 %reduce-scatter.7.cloned.1.call-done = bf16[128,4096]{1,0:T(8,128)(2,1)} async-done(((bf16[256,4096]{1,0:T(8,128)(2,1)}), bf16[128,4096]{1,0:T(8,128)(2,1)}) %reduce-scatter.7.cloned.1.call-update) | async-done | bytes 1048592 | tf_op jit(solution)/shard_map/while/body/eval_jaxpr/reduce_scatter | solution.py:81
  667.1 25.1 %all-reduce.2.cloned.1.call-done = bf16[128,1024]{1,0:T(8,128)(2,1)} async-done(((bf16[128,1024]{1,0:T(8,128)(2,1)}), bf16[128,1024]{1,0:T(8,128)(2,1)}) %all-reduce.2.cloned.1.call-update) | async-done | bytes 262160 | tf_op jit(solution)/shard_map/while/body/eval_jaxpr/psum | solution.py:94
  694.2 5.0 all_gather.81
  699.1 5.0 all_gather.80
  704.1 10.6 reduce-scatter.9.cloned.1.call-done
  719.7 21.4 %all-gather.9.cloned.1.call-done = bf16[256,2048]{0,1:T(8,128)(2,1)} async-done(((bf16[128,2048]{0,1:T(8,128)(2,1)}), bf16[256,2048]{0,1:T(8,128)(2,1)}) %all-gather.9.cloned.1.call-update) | async-done | bytes 1048592 | tf_op jit(solution)/shard_map/while/body/eval_jaxpr/all_gather | solution.py:138
  741.1 34.4 %all-gather.11.cloned.1.call-done = bf16[256,4096]{0,1:T(8,128)(2,1)} async-done(((bf16[256,2048]{0,1:T(8,128)(2,1)}), bf16[256,4096]{0,1:T(8,128)(2,1)}) %all-gather.11.cloned.1.call-update) | async-done | bytes 2097168 | tf_op jit(solution)/shard_map/while/body/eval_jaxpr/all_gather | solution.py:139
  775.5 10.9 convolution_convert_fusion.8
  786.4 16.2 %all_to_all.48 = bf16[2,128,2048]{2,1,0:T(8,128)(2,1)S(1)} all-to-all(bf16[2,128,2048]{2,1,0:T(8,128)(2,1)S(1)} %bitcast.132), channel_id=1, replica_groups=mesh['section'=4,'gx'=2,'gy'=2,'gz'=2] {'gy'}, dimensions={0} | all-to-all | bytes 2097152 | tf_op jit(solution)/shard_map/while/body/eval_jaxpr/all_to_all | solution.py:140
  803.7 7.6 reduce-scatter.11.cloned.1.call-done
  816.4 11.6 %collective-permute-done = bf16[128,2048]{1,0:T(8,128)(2,1)S(1)} collective-permute-done((bf16[128,2048]{1,0:T(8,128)(2,1)S(1)}, bf16[128,2048]{1,0:T(8,128)(2,1)S(1)}, u32[]{:S(2)}, u32[]{:S(2)}) %collective-permute-start) | collective-permute-done | bytes 524320 | tf_op jit(solution)/shard_map/while/body/eval_jaxpr/ppermute | solution.py:16
  828.9 12.4 %all-gather.5.cloned.1.call-done = bf16[128,4096]{1,0:T(8,128)(2,1)} async-done(((bf16[128,2048]{1,0:T(8,128)(2,1)}), bf16[128,4096]{1,0:T(8,128)(2,1)}) %all-gather.5.cloned.1.call-update) | async-done | bytes 1048592 | tf_op jit(solution)/shard_map/while/body/eval_jaxpr/all_gather | solution.py:162
  842.8 4.9 psum.34
  850.4 34.4 %all-gather.7.cloned.1.call-done = bf16[256,4096]{1,0:T(8,128)(2,1)} async-done(((bf16[128,4096]{1,0:T(8,128)(2,1)}), bf16[256,4096]{1,0:T(8,128)(2,1)}) %all-gather.7.cloned.1.call-update) | async-done | bytes 2097168 | tf_op jit(solution)/shard_map/while/body/eval_jaxpr/all_gather | solution.py:76
  884.7 4.6 convolution_convert_fusion.6
  889.4 12.0 %convolution_convert_fusion.7 = bf16[256,4096]{1,0:T(8,128)(2,1)} fusion(bf16[2048,4096]{1,0:T(8,128)(2,1)} %get-tuple-element.638, bf16[256,4096]{1,0:T(8,128)(2,1)} %all-gather.7.cloned.1.call-done, s32[]{:T(128)} %get-tuple-element.634), kind=kOutput, calls=%fused_computation.2.clone.1 | convolution fusion | flops 4296015872 | bytes 19923456 | tf_op jit(solution)/shard_map/while/body/eval_jaxpr/dot_general | solution.py:78
  904.2 34.1 %reduce-scatter.7.cloned.1.call-done = bf16[128,4096]{1,0:T(8,128)(2,1)} async-done(((bf16[256,4096]{1,0:T(8,128)(2,1)}), bf16[128,4096]{1,0:T(8,128)(2,1)}) %reduce-scatter.7.cloned.1.call-update) | async-done | bytes 1048592 | tf_op jit(solution)/shard_map/while/body/eval_jaxpr/reduce_scatter | solution.py:81
  938.8 25.1 %all-reduce.2.cloned.1.call-done = bf16[128,1024]{1,0:T(8,128)(2,1)} async-done(((bf16[128,1024]{1,0:T(8,128)(2,1)}), bf16[128,1024]{1,0:T(8,128)(2,1)}) %all-reduce.2.cloned.1.call-update) | async-done | bytes 262160 | tf_op jit(solution)/shard_map/while/body/eval_jaxpr/psum | solution.py:94
  965.9 5.0 all_gather.81
  970.9 5.0 all_gather.80
  975.9 10.6 reduce-scatter.9.cloned.1.call-done
  991.4 21.4 %all-gather.9.cloned.1.call-done = bf16[256,2048]{0,1:T(8,128)(2,1)} async-done(((bf16[128,2048]{0,1:T(8,128)(2,1)}), bf16[256,2048]{0,1:T(8,128)(2,1)}) %all-gather.9.cloned.1.call-update) | async-done | bytes 1048592 | tf_op jit(solution)/shard_map/while/body/eval_jaxpr/all_gather | solution.py:138
  1012.8 34.6 %all-gather.11.cloned.1.call-done = bf16[256,4096]{0,1:T(8,128)(2,1)} async-done(((bf16[256,2048]{0,1:T(8,128)(2,1)}), bf16[256,4096]{0,1:T(8,128)(2,1)}) %all-gather.11.cloned.1.call-update) | async-done | bytes 2097168 | tf_op jit(solution)/shard_map/while/body/eval_jaxpr/all_gather | solution.py:139
  1047.4 10.9 convolution_convert_fusion.8
  1058.3 16.2 %all_to_all.48 = bf16[2,128,2048]{2,1,0:T(8,128)(2,1)S(1)} all-to-all(bf16[2,128,2048]{2,1,0:T(8,128)(2,1)S(1)} %bitcast.132), channel_id=1, replica_groups=mesh['section'=4,'gx'=2,'gy'=2,'gz'=2] {'gy'}, dimensions={0} | all-to-all | bytes 2097152 | tf_op jit(solution)/shard_map/while/body/eval_jaxpr/all_to_all | solution.py:140
  1075.6 7.6 reduce-scatter.11.cloned.1.call-done
  1088.3 11.6 %collective-permute-done = bf16[128,2048]{1,0:T(8,128)(2,1)S(1)} collective-permute-done((bf16[128,2048]{1,0:T(8,128)(2,1)S(1)}, bf16[128,2048]{1,0:T(8,128)(2,1)S(1)}, u32[]{:S(2)}, u32[]{:S(2)}) %collective-permute-start) | collective-permute-done | bytes 524320 | tf_op jit(solution)/shard_map/while/body/eval_jaxpr/ppermute | solution.py:16
  (222 shorter events, 96.5 us)
Async XLA Ops:
  6.5 0.7 copy-start
  9.8 2.8 copy-start.4
  9.8 2.8 copy-start.5
  9.8 2.8 copy-start.6
  12.6 14.1 %all-gather.5.cloned.1.call-start = ((), (), s32[]{:S(2)}) async-start(), calls=%async_computation.5 | async-start | bytes 1572864 | tf_op jit(solution)/shard_map/while/body/eval_jaxpr/all_gather | solution.py:162
  13.5 56.7 %all-gather.7.cloned.1.call-start = ((), (), s32[]{:S(2)}) async-start(), calls=%async_computation.6 | async-start | bytes 3145728 | tf_op jit(solution)/shard_map/while/body/eval_jaxpr/all_gather | solution.py:76
  35.7 53.9 %reduce-scatter.5.cloned.1.call-start = ((), (), s32[]{:S(2)}) async-start(), calls=%async_computation.7 | async-start | bytes 786432 | tf_op jit(solution)/shard_map/while/body/eval_jaxpr/reduce_scatter | solution.py:84
  74.8 48.8 %reduce-scatter.7.cloned.1.call-start = ((), (), s32[]{:S(2)}) async-start(), calls=%async_computation.9 | async-start | bytes 3145728 | tf_op jit(solution)/shard_map/while/body/eval_jaxpr/reduce_scatter | solution.py:81
  86.8 62.2 %all-reduce.2.cloned.1.call-start = ((), (), s32[]{:S(2)}) async-start(), calls=%async_computation.8 | async-start | bytes 524288 | tf_op jit(solution)/shard_map/while/body/eval_jaxpr/psum | solution.py:94
  89.6 82.0 %reduce-scatter.9.cloned.1.call-start = ((), (), s32[]{:S(2)}) async-start(), calls=%async_computation.10 | async-start | bytes 1572864 | tf_op jit(solution)/shard_map/while/body/eval_jaxpr/reduce_scatter | solution.py:89
  123.7 74.2 %all-gather.9.cloned.1.call-start = ((), (), s32[]{:S(2)}) async-start(), calls=%async_computation.11 | async-start | bytes 1572864 | tf_op jit(solution)/shard_map/while/body/eval_jaxpr/all_gather | solution.py:138
  176.5 56.1 %all-gather.11.cloned.1.call-start = ((), (), s32[]{:S(2)}) async-start(), calls=%async_computation.12 | async-start | bytes 3145728 | tf_op jit(solution)/shard_map/while/body/eval_jaxpr/all_gather | solution.py:139
  197.9 70.4 %reduce-scatter.11.cloned.1.call-start = ((), (), s32[]{:S(2)}) async-start(), calls=%async_computation.13 | async-start | bytes 1572864 | tf_op jit(solution)/shard_map/while/body/eval_jaxpr/reduce_scatter | solution.py:163
  259.6 8.7 copy-start.2
  269.7 15.3 %collective-permute-start = (bf16[128,2048]{1,0:T(8,128)(2,1)S(1)}, bf16[128,2048]{1,0:T(8,128)(2,1)S(1)}, u32[]{:S(2)}, u32[]{:S(2)}) collective-permute-start(bf16[128,2048]{1,0:T(8,128)(2,1)S(1)} %get-tuple-element.592), channel_id=1, source_target_pairs={{0,8},{8,16},{16,24},{1,9},{9,17},{17,25},{2,10},{10,18},{18,26},{... | collective-permute-start | bytes 1572872 | tf_op jit(solution)/shard_map/while/body/eval_jaxpr/ppermute | solution.py:16
  285.0 13.0 %all-gather.5.cloned.1.call-start = ((), (), s32[]{:S(2)}) async-start(), calls=%async_computation.5 | async-start | bytes 1572864 | tf_op jit(solution)/shard_map/while/body/eval_jaxpr/all_gather | solution.py:162
  285.8 55.6 %all-gather.7.cloned.1.call-start = ((), (), s32[]{:S(2)}) async-start(), calls=%async_computation.6 | async-start | bytes 3145728 | tf_op jit(solution)/shard_map/while/body/eval_jaxpr/all_gather | solution.py:76
  307.0 53.9 %reduce-scatter.5.cloned.1.call-start = ((), (), s32[]{:S(2)}) async-start(), calls=%async_computation.7 | async-start | bytes 786432 | tf_op jit(solution)/shard_map/while/body/eval_jaxpr/reduce_scatter | solution.py:84
  346.1 49.0 %reduce-scatter.7.cloned.1.call-start = ((), (), s32[]{:S(2)}) async-start(), calls=%async_computation.9 | async-start | bytes 3145728 | tf_op jit(solution)/shard_map/while/body/eval_jaxpr/reduce_scatter | solution.py:81
  358.1 62.4 %all-reduce.2.cloned.1.call-start = ((), (), s32[]{:S(2)}) async-start(), calls=%async_computation.8 | async-start | bytes 524288 | tf_op jit(solution)/shard_map/while/body/eval_jaxpr/psum | solution.py:94
  360.9 82.1 %reduce-scatter.9.cloned.1.call-start = ((), (), s32[]{:S(2)}) async-start(), calls=%async_computation.10 | async-start | bytes 1572864 | tf_op jit(solution)/shard_map/while/body/eval_jaxpr/reduce_scatter | solution.py:89
  395.1 74.2 %all-gather.9.cloned.1.call-start = ((), (), s32[]{:S(2)}) async-start(), calls=%async_computation.11 | async-start | bytes 1572864 | tf_op jit(solution)/shard_map/while/body/eval_jaxpr/all_gather | solution.py:138
  447.9 55.9 %all-gather.11.cloned.1.call-start = ((), (), s32[]{:S(2)}) async-start(), calls=%async_computation.12 | async-start | bytes 3145728 | tf_op jit(solution)/shard_map/while/body/eval_jaxpr/all_gather | solution.py:139
  469.3 70.3 %reduce-scatter.11.cloned.1.call-start = ((), (), s32[]{:S(2)}) async-start(), calls=%async_computation.13 | async-start | bytes 1572864 | tf_op jit(solution)/shard_map/while/body/eval_jaxpr/reduce_scatter | solution.py:163
  530.9 8.7 copy-start.2
  540.9 15.3 %collective-permute-start = (bf16[128,2048]{1,0:T(8,128)(2,1)S(1)}, bf16[128,2048]{1,0:T(8,128)(2,1)S(1)}, u32[]{:S(2)}, u32[]{:S(2)}) collective-permute-start(bf16[128,2048]{1,0:T(8,128)(2,1)S(1)} %get-tuple-element.592), channel_id=1, source_target_pairs={{0,8},{8,16},{16,24},{1,9},{9,17},{17,25},{2,10},{10,18},{18,26},{... | collective-permute-start | bytes 1572872 | tf_op jit(solution)/shard_map/while/body/eval_jaxpr/ppermute | solution.py:16
  556.2 13.3 %all-gather.5.cloned.1.call-start = ((), (), s32[]{:S(2)}) async-start(), calls=%async_computation.5 | async-start | bytes 1572864 | tf_op jit(solution)/shard_map/while/body/eval_jaxpr/all_gather | solution.py:162
  557.1 55.9 %all-gather.7.cloned.1.call-start = ((), (), s32[]{:S(2)}) async-start(), calls=%async_computation.6 | async-start | bytes 3145728 | tf_op jit(solution)/shard_map/while/body/eval_jaxpr/all_gather | solution.py:76
  578.6 53.9 %reduce-scatter.5.cloned.1.call-start = ((), (), s32[]{:S(2)}) async-start(), calls=%async_computation.7 | async-start | bytes 786432 | tf_op jit(solution)/shard_map/while/body/eval_jaxpr/reduce_scatter | solution.py:84
  617.6 49.0 %reduce-scatter.7.cloned.1.call-start = ((), (), s32[]{:S(2)}) async-start(), calls=%async_computation.9 | async-start | bytes 3145728 | tf_op jit(solution)/shard_map/while/body/eval_jaxpr/reduce_scatter | solution.py:81
  629.7 62.5 %all-reduce.2.cloned.1.call-start = ((), (), s32[]{:S(2)}) async-start(), calls=%async_computation.8 | async-start | bytes 524288 | tf_op jit(solution)/shard_map/while/body/eval_jaxpr/psum | solution.py:94
  632.5 82.3 %reduce-scatter.9.cloned.1.call-start = ((), (), s32[]{:S(2)}) async-start(), calls=%async_computation.10 | async-start | bytes 1572864 | tf_op jit(solution)/shard_map/while/body/eval_jaxpr/reduce_scatter | solution.py:89
  666.6 74.4 %all-gather.9.cloned.1.call-start = ((), (), s32[]{:S(2)}) async-start(), calls=%async_computation.11 | async-start | bytes 1572864 | tf_op jit(solution)/shard_map/while/body/eval_jaxpr/all_gather | solution.py:138
  719.6 55.9 %all-gather.11.cloned.1.call-start = ((), (), s32[]{:S(2)}) async-start(), calls=%async_computation.12 | async-start | bytes 3145728 | tf_op jit(solution)/shard_map/while/body/eval_jaxpr/all_gather | solution.py:139
  741.0 70.3 %reduce-scatter.11.cloned.1.call-start = ((), (), s32[]{:S(2)}) async-start(), calls=%async_computation.13 | async-start | bytes 1572864 | tf_op jit(solution)/shard_map/while/body/eval_jaxpr/reduce_scatter | solution.py:163
  802.6 8.7 copy-start.2
  812.7 15.3 %collective-permute-start = (bf16[128,2048]{1,0:T(8,128)(2,1)S(1)}, bf16[128,2048]{1,0:T(8,128)(2,1)S(1)}, u32[]{:S(2)}, u32[]{:S(2)}) collective-permute-start(bf16[128,2048]{1,0:T(8,128)(2,1)S(1)} %get-tuple-element.592), channel_id=1, source_target_pairs={{0,8},{8,16},{16,24},{1,9},{9,17},{17,25},{2,10},{10,18},{18,26},{... | collective-permute-start | bytes 1572872 | tf_op jit(solution)/shard_map/while/body/eval_jaxpr/ppermute | solution.py:16
  827.9 13.3 %all-gather.5.cloned.1.call-start = ((), (), s32[]{:S(2)}) async-start(), calls=%async_computation.5 | async-start | bytes 1572864 | tf_op jit(solution)/shard_map/while/body/eval_jaxpr/all_gather | solution.py:162
  828.8 55.9 %all-gather.7.cloned.1.call-start = ((), (), s32[]{:S(2)}) async-start(), calls=%async_computation.6 | async-start | bytes 3145728 | tf_op jit(solution)/shard_map/while/body/eval_jaxpr/all_gather | solution.py:76
  850.3 53.9 %reduce-scatter.5.cloned.1.call-start = ((), (), s32[]{:S(2)}) async-start(), calls=%async_computation.7 | async-start | bytes 786432 | tf_op jit(solution)/shard_map/while/body/eval_jaxpr/reduce_scatter | solution.py:84
  889.4 49.0 %reduce-scatter.7.cloned.1.call-start = ((), (), s32[]{:S(2)}) async-start(), calls=%async_computation.9 | async-start | bytes 3145728 | tf_op jit(solution)/shard_map/while/body/eval_jaxpr/reduce_scatter | solution.py:81
  901.4 62.5 %all-reduce.2.cloned.1.call-start = ((), (), s32[]{:S(2)}) async-start(), calls=%async_computation.8 | async-start | bytes 524288 | tf_op jit(solution)/shard_map/while/body/eval_jaxpr/psum | solution.py:94
  904.2 82.3 %reduce-scatter.9.cloned.1.call-start = ((), (), s32[]{:S(2)}) async-start(), calls=%async_computation.10 | async-start | bytes 1572864 | tf_op jit(solution)/shard_map/while/body/eval_jaxpr/reduce_scatter | solution.py:89
  938.4 74.4 %all-gather.9.cloned.1.call-start = ((), (), s32[]{:S(2)}) async-start(), calls=%async_computation.11 | async-start | bytes 1572864 | tf_op jit(solution)/shard_map/while/body/eval_jaxpr/all_gather | solution.py:138
  991.4 56.1 %all-gather.11.cloned.1.call-start = ((), (), s32[]{:S(2)}) async-start(), calls=%async_computation.12 | async-start | bytes 3145728 | tf_op jit(solution)/shard_map/while/body/eval_jaxpr/all_gather | solution.py:139
  1012.8 70.4 %reduce-scatter.11.cloned.1.call-start = ((), (), s32[]{:S(2)}) async-start(), calls=%async_computation.13 | async-start | bytes 1572864 | tf_op jit(solution)/shard_map/while/body/eval_jaxpr/reduce_scatter | solution.py:163
  1074.5 8.7 copy-start.2
  1084.6 15.3 %collective-permute-start = (bf16[128,2048]{1,0:T(8,128)(2,1)S(1)}, bf16[128,2048]{1,0:T(8,128)(2,1)S(1)}, u32[]{:S(2)}, u32[]{:S(2)}) collective-permute-start(bf16[128,2048]{1,0:T(8,128)(2,1)S(1)} %get-tuple-element.592), channel_id=1, source_target_pairs={{0,8},{8,16},{16,24},{1,9},{9,17},{17,25},{2,10},{10,18},{18,26},{... | collective-permute-start | bytes 1572872 | tf_op jit(solution)/shard_map/while/body/eval_jaxpr/ppermute | solution.py:16
  1099.8 0.8 copy-start.3
  1099.8 0.8 copy-start.1
Sparse Core Ops, SparseCore 0:
  14.9 11.7 all-gather.4
  35.8 34.2 all-gather.6
  74.9 14.6 reduce-scatter.4
  91.7 31.8 reduce-scatter.6
  125.7 23.2 all-reduce.1
  151.2 20.3 reduce-scatter.8
  176.6 21.2 all-gather.8
  199.4 33.0 all-gather.10
  260.8 7.4 reduce-scatter.10
  287.0 10.9 all-gather.4
  307.1 34.2 all-gather.6
  346.2 14.6 reduce-scatter.4
  363.1 31.8 reduce-scatter.6
  397.2 23.2 all-reduce.1
  422.6 20.3 reduce-scatter.8
  448.0 21.2 all-gather.8
  470.7 33.0 all-gather.10
  532.1 7.4 reduce-scatter.10
  558.6 10.9 all-gather.4
  578.7 34.2 all-gather.6
  617.7 14.6 reduce-scatter.4
  634.7 31.8 reduce-scatter.6
  668.9 23.2 all-reduce.1
  694.3 20.3 reduce-scatter.8
  719.7 21.2 all-gather.8
  742.4 33.0 all-gather.10
  803.8 7.4 reduce-scatter.10
  830.3 10.9 all-gather.4
  850.4 34.2 all-gather.6
  889.5 14.6 reduce-scatter.4
  906.4 31.8 reduce-scatter.6
  940.6 23.2 all-reduce.1
  966.1 20.3 reduce-scatter.8
  991.5 21.2 all-gather.8
  1014.3 33.0 all-gather.10
  1075.7 7.4 reduce-scatter.10
where the time goes:
time: 1110 us
  waiting for transfers between devices  778 us (70%)
  blocking collectives  124 us (11%)
  matrix products  118 us (11%)
  other arithmetic  44.3 us (4%)
  starting transfers between devices  16.1 us (1%)
  between operations  13.1 us (1%)
  local copies, waits for them, and re-layouts  11.5 us (1%)
    all_gather x4, waiting for transfers between devices, attention_layer(): lax.all_gather(every_token, 'gx', axis=1, tiled=True)  138 us
    all_gather x4, waiting for transfers between devices, attention_layer(): all_tokens = lax.all_gather(normed, 'gy', axis=0, tiled=True)  138 us
    reduce_scatter x4, waiting for transfers between devices, attention_layer(): lax.psum_scatter(query_part.astype(jnp.bfloat16), 'gy', scatter_dimension...  136 us
    psum x4, waiting for transfers between devices, attention_layer(): lax.psum(pair_local.astype(jnp.bfloat16), 'gx').astype(jnp.float32)  100 us
    all_gather x4, waiting for transfers between devices, attention_layer(): every_token = lax.all_gather(attended, 'gy', axis=0, tiled=True)  85.4 us
    all_to_all x4, blocking collectives, attention_layer(): lax.all_to_all(column_sums.astype(jnp.bfloat16), 'gy', split_axis=0, conc...  64.7 us
    all_gather x4, waiting for transfers between devices, advance(): wide_block = lax.all_gather(current, 'gz', axis=1, tiled=True)  50.1 us
    dot_general x4, matrix products, attention_layer(): jnp.dot(own_slab, query_weight, preferred_element_type=jnp.float32)  47.9 us
  transfers between devices with their start and end apart: 40, of which 40 were waited for; matrix products, arithmetic and copies ran while one was open for 5% of the time, Pallas kernels for 0%

commit v1 on v0

--- a/solution.py
+++ b/solution.py
@@ -8,6 +8,11 @@
 ROPE_BASE = 1000000.0
 EPSILON = 1e-06
 NEG_FILL = -1e30
+
+
+def all_parts(value, axis, dim):
+    parts = lax.all_gather(value, axis)
+    return jnp.concatenate(parts, axis=dim)
 
 
 def from_behind(value, axis, steps):
@@ -136,7 +141,7 @@
             .reshape(local_rows, own_cols)
         )
         every_token = lax.all_gather(attended, "gy", axis=0, tiled=True)
-        column_sums = mix_cols(lax.all_gather(every_token, "gx", axis=1, tiled=True))
+        column_sums = mix_cols(all_parts(every_token, "gx", 1))
         return lax.all_to_all(
             column_sums.astype(jnp.bfloat16), "gy", split_axis=0, concat_axis=1, tiled=True
         ).astype(column_sums.dtype)

time: 1110 us -> 1110 us (level)
  local copies, waits for them, and re-layouts: 11.5 us -> 27 us
  matrix products: 118 us -> 103 us
    reshape x0 -> x8, local copies, waits for them, and re-layouts: none -> 15.4 us  [the longest x4 11.4 us: all_parts(): return jnp.concatenate(parts, axis=dim)]
where the time goes in v1:
time: 1110 us
  waiting for transfers between devices  776 us (70%)
  blocking collectives  124 us (11%)
  matrix products  103 us (9%)
  other arithmetic  48.5 us (4%)
  local copies, waits for them, and re-layouts  27 us (2%)
  starting transfers between devices  16.1 us (1%)
  between operations  13.1 us (1%)
    all_gather x4, waiting for transfers between devices, all_parts(): parts = lax.all_gather(value, axis)  138 us
    all_gather x4, waiting for transfers between devices, attention_layer(): all_tokens = lax.all_gather(normed, 'gy', axis=0, tiled=True)  138 us
    reduce_scatter x4, waiting for transfers between devices, attention_layer(): lax.psum_scatter(query_part.astype(jnp.bfloat16), 'gy', scatter_dimension...  136 us
    psum x4, waiting for transfers between devices, attention_layer(): lax.psum(pair_local.astype(jnp.bfloat16), 'gx').astype(jnp.float32)  100 us
    all_gather x4, waiting for transfers between devices, attention_layer(): every_token = lax.all_gather(attended, 'gy', axis=0, tiled=True)  85.6 us
    all_to_all x4, blocking collectives, attention_layer(): lax.all_to_all(column_sums.astype(jnp.bfloat16), 'gy', split_axis=0, conc...  64.7 us
    ppermute x4, waiting for transfers between devices, from_behind(): lax.ppermute(value, axis, [(source, source + steps) for source in range(i...  46.3 us
    dot_general x4, matrix products, attention_layer(): jnp.dot(own_slab, query_weight, preferred_element_type=jnp.float32)  46 us
  transfers between devices with their start and end apart: 40, of which 40 were waited for; matrix products, arithmetic and copies ran while one was open for 5% of the time, Pallas kernels for 0%

profile of v1, /device:TPU:0, one launch (start us, length us, event | category | flops | bytes accessed | tf_op | source)
XLA Modules:
  0.0 1109.5 jit_solution(17893532414025848726)
XLA Ops:
  12.5 1089.6 %while.19 = (s32[]{:T(128)}, bf16[128,2048]{1,0:T(8,128)(2,1)S(1)}, bf16[1,128,2048]{2,1,0:T(8,128)(2,1)S(1)}, pred[]{:T(512)}, bf16[1,128,2048]{2,1,0:T(8,128)(...) while((s32[]{:T(128)}, bf16[128,2048]{1,0:T(8,128)(2,1)S(1)}, ...), condition=%wide.region_10.11_spmd.clone.clone, body=%wide.region_0.10_spmd.clone.clone.sunk | while | flops 9950043136 | bytes 144149136 | solution.py:176
  14.6 12.1 %all-gather.10.cloned.1.call-done = bf16[128,4096]{1,0:T(8,128)(2,1)} async-done(((bf16[128,2048]{1,0:T(8,128)(2,1)}), bf16[128,4096]{1,0:T(8,128)(2,1)}) %all-gather.10.cloned.1.call-update) | async-done | bytes 1048592 | tf_op jit(solution)/shard_map/while/body/eval_jaxpr/all_gather | solution.py:167
  28.2 4.9 psum.34
  35.8 34.4 %all-gather.12.cloned.1.call-done = bf16[256,4096]{1,0:T(8,128)(2,1)} async-done(((bf16[128,4096]{1,0:T(8,128)(2,1)}), bf16[256,4096]{1,0:T(8,128)(2,1)}) %all-gather.12.cloned.1.call-update) | async-done | bytes 2097168 | tf_op jit(solution)/shard_map/while/body/eval_jaxpr/all_gather | solution.py:81
  70.1 4.7 convolution_convert_fusion.6
  74.9 11.5 %convolution_convert_fusion.7 = bf16[256,4096]{1,0:T(8,128)(2,1)} fusion(bf16[2048,4096]{1,0:T(8,128)(2,1)} %get-tuple-element.638, bf16[256,4096]{1,0:T(8,128)(2,1)S(1)} %copy-done.6, s32[]{:T(128)} %get-tuple-element.634), kind=kOutput, calls=%fused_computation.2.clone.1 | convolution fusion | flops 4296015872 | bytes 19922948 | tf_op jit(solution)/shard_map/while/body/eval_jaxpr/dot_general | solution.py:83
  89.7 34.0 %reduce-scatter.7.cloned.1.call-done = bf16[128,4096]{1,0:T(8,128)(2,1)} async-done(((bf16[256,4096]{1,0:T(8,128)(2,1)}), bf16[128,4096]{1,0:T(8,128)(2,1)}) %reduce-scatter.7.cloned.1.call-update) | async-done | bytes 1048592 | tf_op jit(solution)/shard_map/while/body/eval_jaxpr/reduce_scatter | solution.py:86
  124.2 25.0 %all-reduce.2.cloned.1.call-done = bf16[128,1024]{1,0:T(8,128)(2,1)} async-done(((bf16[128,1024]{1,0:T(8,128)(2,1)}), bf16[128,1024]{1,0:T(8,128)(2,1)}) %all-reduce.2.cloned.1.call-update) | async-done | bytes 262160 | tf_op jit(solution)/shard_map/while/body/eval_jaxpr/psum | solution.py:99
  151.1 5.0 all_gather.88
  156.1 5.0 all_gather.87
  161.0 10.6 reduce-scatter.9.cloned.1.call-done
  176.8 21.4 %all-gather.14.cloned.1.call-done = bf16[256,2048]{1,0:T(8,128)(2,1)} async-done(((bf16[128,2048]{1,0:T(8,128)(2,1)}), bf16[256,2048]{1,0:T(8,128)(2,1)}) %all-gather.14.cloned.1.call-update) | async-done | bytes 1048592 | tf_op jit(solution)/shard_map/while/body/eval_jaxpr/all_gather | solution.py:143
  198.3 34.6 %all-gather.16.cloned.1.call-done = bf16[512,2048]{1,0:T(8,128)(2,1)} async-done(((bf16[256,2048]{1,0:T(8,128)(2,1)}), bf16[512,2048]{1,0:T(8,128)(2,1)}) %all-gather.16.cloned.1.call-update) | async-done | bytes 2097168 | tf_op jit(solution)/shard_map/while/body/eval_jaxpr/all_gather | solution.py:14
  235.7 8.3 convolution_convert_fusion.8
  244.0 16.2 %all_to_all.48 = bf16[2,128,2048]{2,1,0:T(8,128)(2,1)S(1)} all-to-all(bf16[2,128,2048]{2,1,0:T(8,128)(2,1)S(1)} %bitcast.141), channel_id=1, replica_groups=mesh['section'=4,'gx'=2,'gy'=2,'gz'=2] {'gy'}, dimensions={0} | all-to-all | bytes 2097152 | tf_op jit(solution)/shard_map/while/body/eval_jaxpr/all_to_all | solution.py:145
  261.3 7.6 reduce-scatter.11.cloned.1.call-done
  274.0 11.6 %collective-permute-done = bf16[128,2048]{1,0:T(8,128)(2,1)S(1)} collective-permute-done((bf16[128,2048]{1,0:T(8,128)(2,1)S(1)}, bf16[128,2048]{1,0:T(8,128)(2,1)S(1)}, u32[]{:S(2)}, u32[]{:S(2)}) %collective-permute-start) | collective-permute-done | bytes 524320 | tf_op jit(solution)/shard_map/while/body/eval_jaxpr/ppermute | solution.py:21
  287.5 11.1 all-gather.10.cloned.1.call-done
  300.1 4.9 psum.34
  307.6 34.4 %all-gather.12.cloned.1.call-done = bf16[256,4096]{1,0:T(8,128)(2,1)} async-done(((bf16[128,4096]{1,0:T(8,128)(2,1)}), bf16[256,4096]{1,0:T(8,128)(2,1)}) %all-gather.12.cloned.1.call-update) | async-done | bytes 2097168 | tf_op jit(solution)/shard_map/while/body/eval_jaxpr/all_gather | solution.py:81
  342.0 4.7 convolution_convert_fusion.6
  346.8 11.5 %convolution_convert_fusion.7 = bf16[256,4096]{1,0:T(8,128)(2,1)} fusion(bf16[2048,4096]{1,0:T(8,128)(2,1)} %get-tuple-element.638, bf16[256,4096]{1,0:T(8,128)(2,1)S(1)} %copy-done.6, s32[]{:T(128)} %get-tuple-element.634), kind=kOutput, calls=%fused_computation.2.clone.1 | convolution fusion | flops 4296015872 | bytes 19922948 | tf_op jit(solution)/shard_map/while/body/eval_jaxpr/dot_general | solution.py:83
  361.6 34.1 %reduce-scatter.7.cloned.1.call-done = bf16[128,4096]{1,0:T(8,128)(2,1)} async-done(((bf16[256,4096]{1,0:T(8,128)(2,1)}), bf16[128,4096]{1,0:T(8,128)(2,1)}) %reduce-scatter.7.cloned.1.call-update) | async-done | bytes 1048592 | tf_op jit(solution)/shard_map/while/body/eval_jaxpr/reduce_scatter | solution.py:86
  396.2 25.0 %all-reduce.2.cloned.1.call-done = bf16[128,1024]{1,0:T(8,128)(2,1)} async-done(((bf16[128,1024]{1,0:T(8,128)(2,1)}), bf16[128,1024]{1,0:T(8,128)(2,1)}) %all-reduce.2.cloned.1.call-update) | async-done | bytes 262160 | tf_op jit(solution)/shard_map/while/body/eval_jaxpr/psum | solution.py:99
  423.1 5.0 all_gather.88
  428.1 5.0 all_gather.87
  433.0 10.6 reduce-scatter.9.cloned.1.call-done
  448.8 21.4 %all-gather.14.cloned.1.call-done = bf16[256,2048]{1,0:T(8,128)(2,1)} async-done(((bf16[128,2048]{1,0:T(8,128)(2,1)}), bf16[256,2048]{1,0:T(8,128)(2,1)}) %all-gather.14.cloned.1.call-update) | async-done | bytes 1048592 | tf_op jit(solution)/shard_map/while/body/eval_jaxpr/all_gather | solution.py:143
  470.3 34.4 %all-gather.16.cloned.1.call-done = bf16[512,2048]{1,0:T(8,128)(2,1)} async-done(((bf16[256,2048]{1,0:T(8,128)(2,1)}), bf16[512,2048]{1,0:T(8,128)(2,1)}) %all-gather.16.cloned.1.call-update) | async-done | bytes 2097168 | tf_op jit(solution)/shard_map/while/body/eval_jaxpr/all_gather | solution.py:14
  507.6 8.3 convolution_convert_fusion.8
  515.9 16.2 %all_to_all.48 = bf16[2,128,2048]{2,1,0:T(8,128)(2,1)S(1)} all-to-all(bf16[2,128,2048]{2,1,0:T(8,128)(2,1)S(1)} %bitcast.141), channel_id=1, replica_groups=mesh['section'=4,'gx'=2,'gy'=2,'gz'=2] {'gy'}, dimensions={0} | all-to-all | bytes 2097152 | tf_op jit(solution)/shard_map/while/body/eval_jaxpr/all_to_all | solution.py:145
  533.1 7.6 reduce-scatter.11.cloned.1.call-done
  545.8 11.6 %collective-permute-done = bf16[128,2048]{1,0:T(8,128)(2,1)S(1)} collective-permute-done((bf16[128,2048]{1,0:T(8,128)(2,1)S(1)}, bf16[128,2048]{1,0:T(8,128)(2,1)S(1)}, u32[]{:S(2)}, u32[]{:S(2)}) %collective-permute-start) | collective-permute-done | bytes 524320 | tf_op jit(solution)/shard_map/while/body/eval_jaxpr/ppermute | solution.py:21
  559.3 11.4 %all-gather.10.cloned.1.call-done = bf16[128,4096]{1,0:T(8,128)(2,1)} async-done(((bf16[128,2048]{1,0:T(8,128)(2,1)}), bf16[128,4096]{1,0:T(8,128)(2,1)}) %all-gather.10.cloned.1.call-update) | async-done | bytes 1048592 | tf_op jit(solution)/shard_map/while/body/eval_jaxpr/all_gather | solution.py:167
  572.2 4.9 psum.34
  579.8 34.4 %all-gather.12.cloned.1.call-done = bf16[256,4096]{1,0:T(8,128)(2,1)} async-done(((bf16[128,4096]{1,0:T(8,128)(2,1)}), bf16[256,4096]{1,0:T(8,128)(2,1)}) %all-gather.12.cloned.1.call-update) | async-done | bytes 2097168 | tf_op jit(solution)/shard_map/while/body/eval_jaxpr/all_gather | solution.py:81
  618.9 11.5 %convolution_convert_fusion.7 = bf16[256,4096]{1,0:T(8,128)(2,1)} fusion(bf16[2048,4096]{1,0:T(8,128)(2,1)} %get-tuple-element.638, bf16[256,4096]{1,0:T(8,128)(2,1)S(1)} %copy-done.6, s32[]{:T(128)} %get-tuple-element.634), kind=kOutput, calls=%fused_computation.2.clone.1 | convolution fusion | flops 4296015872 | bytes 19922948 | tf_op jit(solution)/shard_map/while/body/eval_jaxpr/dot_general | solution.py:83
  633.7 34.1 %reduce-scatter.7.cloned.1.call-done = bf16[128,4096]{1,0:T(8,128)(2,1)} async-done(((bf16[256,4096]{1,0:T(8,128)(2,1)}), bf16[128,4096]{1,0:T(8,128)(2,1)}) %reduce-scatter.7.cloned.1.call-update) | async-done | bytes 1048592 | tf_op jit(solution)/shard_map/while/body/eval_jaxpr/reduce_scatter | solution.py:86
  668.3 25.1 %all-reduce.2.cloned.1.call-done = bf16[128,1024]{1,0:T(8,128)(2,1)} async-done(((bf16[128,1024]{1,0:T(8,128)(2,1)}), bf16[128,1024]{1,0:T(8,128)(2,1)}) %all-reduce.2.cloned.1.call-update) | async-done | bytes 262160 | tf_op jit(solution)/shard_map/while/body/eval_jaxpr/psum | solution.py:99
  695.4 5.0 all_gather.88
  700.4 5.0 all_gather.87
  705.3 10.6 reduce-scatter.9.cloned.1.call-done
  721.1 21.4 %all-gather.14.cloned.1.call-done = bf16[256,2048]{1,0:T(8,128)(2,1)} async-done(((bf16[128,2048]{1,0:T(8,128)(2,1)}), bf16[256,2048]{1,0:T(8,128)(2,1)}) %all-gather.14.cloned.1.call-update) | async-done | bytes 1048592 | tf_op jit(solution)/shard_map/while/body/eval_jaxpr/all_gather | solution.py:143
  742.6 34.4 %all-gather.16.cloned.1.call-done = bf16[512,2048]{1,0:T(8,128)(2,1)} async-done(((bf16[256,2048]{1,0:T(8,128)(2,1)}), bf16[512,2048]{1,0:T(8,128)(2,1)}) %all-gather.16.cloned.1.call-update) | async-done | bytes 2097168 | tf_op jit(solution)/shard_map/while/body/eval_jaxpr/all_gather | solution.py:14
  779.9 8.3 convolution_convert_fusion.8
  788.2 16.2 %all_to_all.48 = bf16[2,128,2048]{2,1,0:T(8,128)(2,1)S(1)} all-to-all(bf16[2,128,2048]{2,1,0:T(8,128)(2,1)S(1)} %bitcast.141), channel_id=1, replica_groups=mesh['section'=4,'gx'=2,'gy'=2,'gz'=2] {'gy'}, dimensions={0} | all-to-all | bytes 2097152 | tf_op jit(solution)/shard_map/while/body/eval_jaxpr/all_to_all | solution.py:145
  805.4 7.6 reduce-scatter.11.cloned.1.call-done
  818.1 11.6 %collective-permute-done = bf16[128,2048]{1,0:T(8,128)(2,1)S(1)} collective-permute-done((bf16[128,2048]{1,0:T(8,128)(2,1)S(1)}, bf16[128,2048]{1,0:T(8,128)(2,1)S(1)}, u32[]{:S(2)}, u32[]{:S(2)}) %collective-permute-start) | collective-permute-done | bytes 524320 | tf_op jit(solution)/shard_map/while/body/eval_jaxpr/ppermute | solution.py:21
  831.7 11.3 %all-gather.10.cloned.1.call-done = bf16[128,4096]{1,0:T(8,128)(2,1)} async-done(((bf16[128,2048]{1,0:T(8,128)(2,1)}), bf16[128,4096]{1,0:T(8,128)(2,1)}) %all-gather.10.cloned.1.call-update) | async-done | bytes 1048592 | tf_op jit(solution)/shard_map/while/body/eval_jaxpr/all_gather | solution.py:167
  844.5 4.9 psum.34
  852.1 34.4 %all-gather.12.cloned.1.call-done = bf16[256,4096]{1,0:T(8,128)(2,1)} async-done(((bf16[128,4096]{1,0:T(8,128)(2,1)}), bf16[256,4096]{1,0:T(8,128)(2,1)}) %all-gather.12.cloned.1.call-update) | async-done | bytes 2097168 | tf_op jit(solution)/shard_map/while/body/eval_jaxpr/all_gather | solution.py:81
  886.5 4.7 convolution_convert_fusion.6
  891.3 11.5 %convolution_convert_fusion.7 = bf16[256,4096]{1,0:T(8,128)(2,1)} fusion(bf16[2048,4096]{1,0:T(8,128)(2,1)} %get-tuple-element.638, bf16[256,4096]{1,0:T(8,128)(2,1)S(1)} %copy-done.6, s32[]{:T(128)} %get-tuple-element.634), kind=kOutput, calls=%fused_computation.2.clone.1 | convolution fusion | flops 4296015872 | bytes 19922948 | tf_op jit(solution)/shard_map/while/body/eval_jaxpr/dot_general | solution.py:83
  906.1 34.1 %reduce-scatter.7.cloned.1.call-done = bf16[128,4096]{1,0:T(8,128)(2,1)} async-done(((bf16[256,4096]{1,0:T(8,128)(2,1)}), bf16[128,4096]{1,0:T(8,128)(2,1)}) %reduce-scatter.7.cloned.1.call-update) | async-done | bytes 1048592 | tf_op jit(solution)/shard_map/while/body/eval_jaxpr/reduce_scatter | solution.py:86
  940.7 25.1 %all-reduce.2.cloned.1.call-done = bf16[128,1024]{1,0:T(8,128)(2,1)} async-done(((bf16[128,1024]{1,0:T(8,128)(2,1)}), bf16[128,1024]{1,0:T(8,128)(2,1)}) %all-reduce.2.cloned.1.call-update) | async-done | bytes 262160 | tf_op jit(solution)/shard_map/while/body/eval_jaxpr/psum | solution.py:99
  967.8 5.0 all_gather.88
  972.7 5.0 all_gather.87
  977.7 10.6 reduce-scatter.9.cloned.1.call-done
  993.4 21.4 %all-gather.14.cloned.1.call-done = bf16[256,2048]{1,0:T(8,128)(2,1)} async-done(((bf16[128,2048]{1,0:T(8,128)(2,1)}), bf16[256,2048]{1,0:T(8,128)(2,1)}) %all-gather.14.cloned.1.call-update) | async-done | bytes 1048592 | tf_op jit(solution)/shard_map/while/body/eval_jaxpr/all_gather | solution.py:143
  1014.9 34.6 %all-gather.16.cloned.1.call-done = bf16[512,2048]{1,0:T(8,128)(2,1)} async-done(((bf16[256,2048]{1,0:T(8,128)(2,1)}), bf16[512,2048]{1,0:T(8,128)(2,1)}) %all-gather.16.cloned.1.call-update) | async-done | bytes 2097168 | tf_op jit(solution)/shard_map/while/body/eval_jaxpr/all_gather | solution.py:14
  1052.3 8.3 convolution_convert_fusion.8
  1060.7 16.2 %all_to_all.48 = bf16[2,128,2048]{2,1,0:T(8,128)(2,1)S(1)} all-to-all(bf16[2,128,2048]{2,1,0:T(8,128)(2,1)S(1)} %bitcast.141), channel_id=1, replica_groups=mesh['section'=4,'gx'=2,'gy'=2,'gz'=2] {'gy'}, dimensions={0} | all-to-all | bytes 2097152 | tf_op jit(solution)/shard_map/while/body/eval_jaxpr/all_to_all | solution.py:145
  1077.9 7.6 reduce-scatter.11.cloned.1.call-done
  1090.6 11.6 %collective-permute-done = bf16[128,2048]{1,0:T(8,128)(2,1)S(1)} collective-permute-done((bf16[128,2048]{1,0:T(8,128)(2,1)S(1)}, bf16[128,2048]{1,0:T(8,128)(2,1)S(1)}, u32[]{:S(2)}, u32[]{:S(2)}) %collective-permute-start) | collective-permute-done | bytes 524320 | tf_op jit(solution)/shard_map/while/body/eval_jaxpr/ppermute | solution.py:21
  (236 shorter events, 114.8 us)
Async XLA Ops:
  6.5 0.7 copy-start
  9.8 2.8 copy-start.4
  9.8 2.8 copy-start.5
  12.5 14.1 %all-gather.10.cloned.1.call-start = ((), (), s32[]{:S(2)}) async-start(), calls=%async_computation.5 | async-start | bytes 1572864 | tf_op jit(solution)/shard_map/while/body/eval_jaxpr/all_gather | solution.py:167
  14.5 55.6 %all-gather.12.cloned.1.call-start = ((), (), s32[]{:S(2)}) async-start(), calls=%async_computation.6 | async-start | bytes 3145728 | tf_op jit(solution)/shard_map/while/body/eval_jaxpr/all_gather | solution.py:81
  35.7 54.0 %reduce-scatter.5.cloned.1.call-start = ((), (), s32[]{:S(2)}) async-start(), calls=%async_computation.7 | async-start | bytes 786432 | tf_op jit(solution)/shard_map/while/body/eval_jaxpr/reduce_scatter | solution.py:89
  70.1 4.8 copy-start.6
  74.9 48.8 %reduce-scatter.7.cloned.1.call-start = ((), (), s32[]{:S(2)}) async-start(), calls=%async_computation.9 | async-start | bytes 3145728 | tf_op jit(solution)/shard_map/while/body/eval_jaxpr/reduce_scatter | solution.py:86
  86.5 62.7 %all-reduce.2.cloned.1.call-start = ((), (), s32[]{:S(2)}) async-start(), calls=%async_computation.8 | async-start | bytes 524288 | tf_op jit(solution)/shard_map/while/body/eval_jaxpr/psum | solution.py:99
  89.7 82.0 %reduce-scatter.9.cloned.1.call-start = ((), (), s32[]{:S(2)}) async-start(), calls=%async_computation.10 | async-start | bytes 1572864 | tf_op jit(solution)/shard_map/while/body/eval_jaxpr/reduce_scatter | solution.py:94
  123.7 74.5 %all-gather.14.cloned.1.call-start = ((), (), s32[]{:S(2)}) async-start(), calls=%async_computation.11 | async-start | bytes 1572864 | tf_op jit(solution)/shard_map/while/body/eval_jaxpr/all_gather | solution.py:143
  176.7 56.1 %all-gather.16.cloned.1.call-start = ((), (), s32[]{:S(2)}) async-start(), calls=%async_computation.12 | async-start | bytes 3145728 | tf_op jit(solution)/shard_map/while/body/eval_jaxpr/all_gather | solution.py:14
  198.2 70.7 %reduce-scatter.11.cloned.1.call-start = ((), (), s32[]{:S(2)}) async-start(), calls=%async_computation.13 | async-start | bytes 1572864 | tf_op jit(solution)/shard_map/while/body/eval_jaxpr/reduce_scatter | solution.py:168
  260.2 8.7 copy-start.2
  270.2 15.3 %collective-permute-start = (bf16[128,2048]{1,0:T(8,128)(2,1)S(1)}, bf16[128,2048]{1,0:T(8,128)(2,1)S(1)}, u32[]{:S(2)}, u32[]{:S(2)}) collective-permute-start(bf16[128,2048]{1,0:T(8,128)(2,1)S(1)} %get-tuple-element.592), channel_id=1, source_target_pairs={{0,8},{8,16},{16,24},{1,9},{9,17},{17,25},{2,10},{10,18},{18,26},{... | collective-permute-start | bytes 1572872 | tf_op jit(solution)/shard_map/while/body/eval_jaxpr/ppermute | solution.py:21
  285.5 13.0 %all-gather.10.cloned.1.call-start = ((), (), s32[]{:S(2)}) async-start(), calls=%async_computation.5 | async-start | bytes 1572864 | tf_op jit(solution)/shard_map/while/body/eval_jaxpr/all_gather | solution.py:167
  287.4 54.6 %all-gather.12.cloned.1.call-start = ((), (), s32[]{:S(2)}) async-start(), calls=%async_computation.6 | async-start | bytes 3145728 | tf_op jit(solution)/shard_map/while/body/eval_jaxpr/all_gather | solution.py:81
  307.6 54.0 %reduce-scatter.5.cloned.1.call-start = ((), (), s32[]{:S(2)}) async-start(), calls=%async_computation.7 | async-start | bytes 786432 | tf_op jit(solution)/shard_map/while/body/eval_jaxpr/reduce_scatter | solution.py:89
  342.0 4.8 copy-start.6
  346.7 49.0 %reduce-scatter.7.cloned.1.call-start = ((), (), s32[]{:S(2)}) async-start(), calls=%async_computation.9 | async-start | bytes 3145728 | tf_op jit(solution)/shard_map/while/body/eval_jaxpr/reduce_scatter | solution.py:86
  358.3 62.8 %all-reduce.2.cloned.1.call-start = ((), (), s32[]{:S(2)}) async-start(), calls=%async_computation.8 | async-start | bytes 524288 | tf_op jit(solution)/shard_map/while/body/eval_jaxpr/psum | solution.py:99
  361.5 82.1 %reduce-scatter.9.cloned.1.call-start = ((), (), s32[]{:S(2)}) async-start(), calls=%async_computation.10 | async-start | bytes 1572864 | tf_op jit(solution)/shard_map/while/body/eval_jaxpr/reduce_scatter | solution.py:94
  395.7 74.5 %all-gather.14.cloned.1.call-start = ((), (), s32[]{:S(2)}) async-start(), calls=%async_computation.11 | async-start | bytes 1572864 | tf_op jit(solution)/shard_map/while/body/eval_jaxpr/all_gather | solution.py:143
  448.7 56.0 %all-gather.16.cloned.1.call-start = ((), (), s32[]{:S(2)}) async-start(), calls=%async_computation.12 | async-start | bytes 3145728 | tf_op jit(solution)/shard_map/while/body/eval_jaxpr/all_gather | solution.py:14
  470.2 70.5 %reduce-scatter.11.cloned.1.call-start = ((), (), s32[]{:S(2)}) async-start(), calls=%async_computation.13 | async-start | bytes 1572864 | tf_op jit(solution)/shard_map/while/body/eval_jaxpr/reduce_scatter | solution.py:168
  532.0 8.7 copy-start.2
  542.1 15.3 %collective-permute-start = (bf16[128,2048]{1,0:T(8,128)(2,1)S(1)}, bf16[128,2048]{1,0:T(8,128)(2,1)S(1)}, u32[]{:S(2)}, u32[]{:S(2)}) collective-permute-start(bf16[128,2048]{1,0:T(8,128)(2,1)S(1)} %get-tuple-element.592), channel_id=1, source_target_pairs={{0,8},{8,16},{16,24},{1,9},{9,17},{17,25},{2,10},{10,18},{18,26},{... | collective-permute-start | bytes 1572872 | tf_op jit(solution)/shard_map/while/body/eval_jaxpr/ppermute | solution.py:21
  557.4 13.3 %all-gather.10.cloned.1.call-start = ((), (), s32[]{:S(2)}) async-start(), calls=%async_computation.5 | async-start | bytes 1572864 | tf_op jit(solution)/shard_map/while/body/eval_jaxpr/all_gather | solution.py:167
  559.3 54.9 %all-gather.12.cloned.1.call-start = ((), (), s32[]{:S(2)}) async-start(), calls=%async_computation.6 | async-start | bytes 3145728 | tf_op jit(solution)/shard_map/while/body/eval_jaxpr/all_gather | solution.py:81
  579.7 54.0 %reduce-scatter.5.cloned.1.call-start = ((), (), s32[]{:S(2)}) async-start(), calls=%async_computation.7 | async-start | bytes 786432 | tf_op jit(solution)/shard_map/while/body/eval_jaxpr/reduce_scatter | solution.py:89
  614.2 4.8 copy-start.6
  618.9 49.0 %reduce-scatter.7.cloned.1.call-start = ((), (), s32[]{:S(2)}) async-start(), calls=%async_computation.9 | async-start | bytes 3145728 | tf_op jit(solution)/shard_map/while/body/eval_jaxpr/reduce_scatter | solution.py:86
  630.5 63.0 %all-reduce.2.cloned.1.call-start = ((), (), s32[]{:S(2)}) async-start(), calls=%async_computation.8 | async-start | bytes 524288 | tf_op jit(solution)/shard_map/while/body/eval_jaxpr/psum | solution.py:99
  633.7 82.3 %reduce-scatter.9.cloned.1.call-start = ((), (), s32[]{:S(2)}) async-start(), calls=%async_computation.10 | async-start | bytes 1572864 | tf_op jit(solution)/shard_map/while/body/eval_jaxpr/reduce_scatter | solution.py:94
  667.9 74.6 %all-gather.14.cloned.1.call-start = ((), (), s32[]{:S(2)}) async-start(), calls=%async_computation.11 | async-start | bytes 1572864 | tf_op jit(solution)/shard_map/while/body/eval_jaxpr/all_gather | solution.py:143
  721.1 56.0 %all-gather.16.cloned.1.call-start = ((), (), s32[]{:S(2)}) async-start(), calls=%async_computation.12 | async-start | bytes 3145728 | tf_op jit(solution)/shard_map/while/body/eval_jaxpr/all_gather | solution.py:14
  742.5 70.5 %reduce-scatter.11.cloned.1.call-start = ((), (), s32[]{:S(2)}) async-start(), calls=%async_computation.13 | async-start | bytes 1572864 | tf_op jit(solution)/shard_map/while/body/eval_jaxpr/reduce_scatter | solution.py:168
  804.3 8.7 copy-start.2
  814.4 15.3 %collective-permute-start = (bf16[128,2048]{1,0:T(8,128)(2,1)S(1)}, bf16[128,2048]{1,0:T(8,128)(2,1)S(1)}, u32[]{:S(2)}, u32[]{:S(2)}) collective-permute-start(bf16[128,2048]{1,0:T(8,128)(2,1)S(1)} %get-tuple-element.592), channel_id=1, source_target_pairs={{0,8},{8,16},{16,24},{1,9},{9,17},{17,25},{2,10},{10,18},{18,26},{... | collective-permute-start | bytes 1572872 | tf_op jit(solution)/shard_map/while/body/eval_jaxpr/ppermute | solution.py:21
  829.7 13.3 %all-gather.10.cloned.1.call-start = ((), (), s32[]{:S(2)}) async-start(), calls=%async_computation.5 | async-start | bytes 1572864 | tf_op jit(solution)/shard_map/while/body/eval_jaxpr/all_gather | solution.py:167
  831.6 54.8 %all-gather.12.cloned.1.call-start = ((), (), s32[]{:S(2)}) async-start(), calls=%async_computation.6 | async-start | bytes 3145728 | tf_op jit(solution)/shard_map/while/body/eval_jaxpr/all_gather | solution.py:81
  852.0 54.0 %reduce-scatter.5.cloned.1.call-start = ((), (), s32[]{:S(2)}) async-start(), calls=%async_computation.7 | async-start | bytes 786432 | tf_op jit(solution)/shard_map/while/body/eval_jaxpr/reduce_scatter | solution.py:89
  886.5 4.8 copy-start.6
  891.2 49.0 %reduce-scatter.7.cloned.1.call-start = ((), (), s32[]{:S(2)}) async-start(), calls=%async_computation.9 | async-start | bytes 3145728 | tf_op jit(solution)/shard_map/while/body/eval_jaxpr/reduce_scatter | solution.py:86
  902.8 63.0 %all-reduce.2.cloned.1.call-start = ((), (), s32[]{:S(2)}) async-start(), calls=%async_computation.8 | async-start | bytes 524288 | tf_op jit(solution)/shard_map/while/body/eval_jaxpr/psum | solution.py:99
  906.0 82.3 %reduce-scatter.9.cloned.1.call-start = ((), (), s32[]{:S(2)}) async-start(), calls=%async_computation.10 | async-start | bytes 1572864 | tf_op jit(solution)/shard_map/while/body/eval_jaxpr/reduce_scatter | solution.py:94
  940.2 74.6 %all-gather.14.cloned.1.call-start = ((), (), s32[]{:S(2)}) async-start(), calls=%async_computation.11 | async-start | bytes 1572864 | tf_op jit(solution)/shard_map/while/body/eval_jaxpr/all_gather | solution.py:143
  993.4 56.1 %all-gather.16.cloned.1.call-start = ((), (), s32[]{:S(2)}) async-start(), calls=%async_computation.12 | async-start | bytes 3145728 | tf_op jit(solution)/shard_map/while/body/eval_jaxpr/all_gather | solution.py:14
  1014.9 70.7 %reduce-scatter.11.cloned.1.call-start = ((), (), s32[]{:S(2)}) async-start(), calls=%async_computation.13 | async-start | bytes 1572864 | tf_op jit(solution)/shard_map/while/body/eval_jaxpr/reduce_scatter | solution.py:168
  1076.8 8.7 copy-start.2
  1086.9 15.3 %collective-permute-start = (bf16[128,2048]{1,0:T(8,128)(2,1)S(1)}, bf16[128,2048]{1,0:T(8,128)(2,1)S(1)}, u32[]{:S(2)}, u32[]{:S(2)}) collective-permute-start(bf16[128,2048]{1,0:T(8,128)(2,1)S(1)} %get-tuple-element.592), channel_id=1, source_target_pairs={{0,8},{8,16},{16,24},{1,9},{9,17},{17,25},{2,10},{10,18},{18,26},{... | collective-permute-start | bytes 1572872 | tf_op jit(solution)/shard_map/while/body/eval_jaxpr/ppermute | solution.py:21
  1102.2 0.8 copy-start.3
  1102.2 0.8 copy-start.1
Sparse Core Ops, SparseCore 0:
  14.9 11.7 all-gather.9
  35.8 34.2 all-gather.11
  75.0 14.6 reduce-scatter.4
  91.8 31.8 reduce-scatter.6
  125.8 23.2 all-reduce.1
  151.2 20.3 reduce-scatter.8
  176.9 21.2 all-gather.13
  199.7 33.0 all-gather.15
  261.4 7.4 reduce-scatter.10
  287.5 10.9 all-gather.9
  307.7 34.2 all-gather.11
  346.8 14.6 reduce-scatter.4
  363.8 31.8 reduce-scatter.6
  397.8 23.2 all-reduce.1
  423.2 20.3 reduce-scatter.8
  448.9 21.2 all-gather.13
  471.6 33.0 all-gather.15
  533.2 7.4 reduce-scatter.10
  559.7 10.9 all-gather.9
  579.8 34.2 all-gather.11
  619.0 14.6 reduce-scatter.4
  635.9 31.8 reduce-scatter.6
  670.1 23.2 all-reduce.1
  695.6 20.3 reduce-scatter.8
  721.2 21.2 all-gather.13
  743.9 33.0 all-gather.15
  805.5 7.4 reduce-scatter.10
  832.1 10.9 all-gather.9
  852.2 34.2 all-gather.11
  891.3 14.6 reduce-scatter.4
  908.2 31.8 reduce-scatter.6
  942.5 23.2 all-reduce.1
  967.9 20.3 reduce-scatter.8
  993.5 21.2 all-gather.13
  1016.4 33.0 all-gather.15
  1078.0 7.4 reduce-scatter.10
